TPU v7x, 32 devices: a whole 2x2x4 slice. The times are simulated.
32 devices in a mesh: dp: 4 (over y, core), tensor: 8 (over z, x).
Axes of the slice: x: 2, y: 2, z: 4, core: 2. Of those that a mesh axis runs over, the one named last changes fastest.
Arguments:
- ref_hidden: bfloat16 [1152, 4608], P('dp', 'tensor'), may hold values from -6 to 6
- pol_hidden: bfloat16 [1152, 4608], P('dp', 'tensor'), may hold values from -6 to 6
- readout: bfloat16 [1152, 4608], P('dp', 'tensor'), may hold values from -0.019897461 to 0.019897461
- lengths: int32 [12], P('dp'), may hold values from 16 to 96, as said below
- pairing: int32 [12], replicated, may hold values from 0 to 11, each once
- pre_gain: float32 [4608], replicated, may hold values from 0.25 to 1.75
- post_gain: float32 [4608], replicated, may hold values from 0.25 to 1.75
- w_query: bfloat16 [4608, 4096], P('dp', 'tensor'), may hold values from -0.09375 to 0.09375
- w_key: bfloat16 [4608, 2048], P('dp', 'tensor'), may hold values from -3 to 3
- value_projection: bfloat16 [4608, 2048], P('dp', 'tensor'), may hold values from -0.09375 to 0.09375
- w_out: bfloat16 [4608, 4096], P('dp', 'tensor'), may hold values from -0.09375 to 0.09375
- a_query: bfloat16 [4608, 64], P('dp'), may hold values from -0.09375 to 0.09375
- a_value: bfloat16 [4608, 64], P('dp'), may hold values from -0.09375 to 0.09375
- query_second_factor: bfloat16 [64, 4096], P(None, 'tensor'), may hold values from -0.75 to 0.75
- value_second_factor: bfloat16 [64, 2048], P(None, 'tensor'), may hold values from -0.75 to 0.75
Outputs:
- policy_out: bfloat16 [1152, 4608], P('dp', 'tensor')
- reference_out: bfloat16 [1152, 4608], P('dp', 'tensor')
- dpo_loss: float32 [], replicated
- grad_hidden: bfloat16 [1152, 4608], P('dp', 'tensor')
- grad_a: float32 [4608, 128], P('dp')
- query_factor_gradient: float32 [64, 4096], P(None, 'tensor')
- value_factor_gradient: float32 [64, 2048], P(None, 'tensor')
Inputs may be any that keep to these rules, and one draw needn't show every extreme that they name: `lengths`: every sequence has at least one valid token and some sequence is full. `pairing`: entries 2k and 2k + 1 name the chosen and the rejected sequence of pair k; every sequence appears once.
All inputs are finite; a program needn't handle non-finite values.
Results may differ from a plain program's by a relative error of at most 0.0233.
The roundings to bfloat16 on the way count: a program that leaves them out, or rounds other values in their place, can miss the bound.
Values may be sent and summed in bfloat16 or wider, within the bound.
A program may use at most 128 MiB of HBM per device.

v0:
```python
import jax
import jax.numpy as jnp
from jax import lax
from jax.sharding import PartitionSpec as P

MODEL_WIDTH = 4608
HQ = 32
HEAD_SIZE = 128
NORM_EPS = 1e-06
SOFT_CAP = 50.0
ADAPTER_SCALE = 0.5
DPO_BETA = 0.5
LOSS_SCALE = 256.0
ROPE_BASE = 10000.0


def query_scale():
    return float(MODEL_WIDTH // HQ) ** (-0.5)


def apply_rotation(value_rows, direction):
    length = value_rows.shape[1]
    head_depth = value_rows.shape[3]
    middle = head_depth // 2
    spacing = ROPE_BASE ** (-2.0 * jnp.arange(middle, dtype=jnp.float32) / head_depth)
    angles = jnp.arange(length, dtype=jnp.float32)[:, None] * spacing[None, :]
    cosine = jnp.cos(angles)[None, :, None, :]
    sine_part = direction * jnp.sin(angles)[None, :, None, :]
    leading = value_rows[..., :middle]
    trailing = value_rows[..., middle:]
    return jnp.concatenate(
        [leading * cosine - trailing * sine_part, trailing * cosine + leading * sine_part], axis=-1
    )


def allowed_mask(lengths, length):
    places = jnp.arange(length)
    causal = places[None, :] <= places[:, None]
    living = places[None, :] < lengths[:, None]
    return causal[None, None, None, :, :] & living[:, None, None, None, :]


def attend(query_rows, rotated_keys, value_rows, lengths):
    seqs_here, length, q_heads, head_depth = query_rows.shape
    kv_heads = rotated_keys.shape[2]
    grouped_heads = query_rows.reshape(seqs_here, length, kv_heads, q_heads // kv_heads, head_depth)
    scores = (
        jnp.einsum(
            "sqkgd,spkd->skgqp", grouped_heads, rotated_keys, preferred_element_type=jnp.float32
        )
        * query_scale()
    )
    capped = SOFT_CAP * jnp.tanh(scores / SOFT_CAP)
    allowed = allowed_mask(lengths, length)
    weights = jnp.where(allowed, jnp.exp(capped), 0.0)
    probabilities = weights / jnp.sum(weights, axis=-1, keepdims=True)
    probs_low = probabilities.astype(jnp.bfloat16)
    mixed_out = jnp.einsum(
        "skgqp,spkd->sqkgd", probs_low, value_rows, preferred_element_type=jnp.float32
    )
    return (
        mixed_out.astype(jnp.bfloat16).reshape(seqs_here, length, q_heads, head_depth),
        probs_low,
        probabilities,
        capped,
    )


def attend_back(grad_mixed, query_rows, rotated_keys, value_rows, probs_low, probabilities, capped):
    seqs_here, length, q_heads, head_depth = query_rows.shape
    kv_heads = rotated_keys.shape[2]
    shape_five = (seqs_here, length, kv_heads, q_heads // kv_heads, head_depth)
    grouped_heads = query_rows.reshape(shape_five)
    grad_grouped = grad_mixed.reshape(shape_five)
    grad_probs = jnp.einsum(
        "sqkgd,spkd->skgqp", grad_grouped, value_rows, preferred_element_type=jnp.float32
    )
    value_rows_gradient = jnp.einsum(
        "skgqp,sqkgd->spkd", probs_low, grad_grouped, preferred_element_type=jnp.float32
    )
    centered = grad_probs - jnp.sum(grad_probs * probabilities, axis=-1, keepdims=True)
    grad_scores = (
        probabilities * centered * (1.0 - (capped / SOFT_CAP) ** 2) * query_scale()
    ).astype(jnp.bfloat16)
    query_rows_gradient = jnp.einsum(
        "skgqp,spkd->sqkgd", grad_scores, rotated_keys, preferred_element_type=jnp.float32
    ).reshape(seqs_here, length, q_heads, head_depth)
    key_rows_gradient = jnp.einsum(
        "skgqp,sqkgd->spkd", grad_scores, grouped_heads, preferred_element_type=jnp.float32
    )
    return (query_rows_gradient, key_rows_gradient, value_rows_gradient)


def normalize(hidden, pre_gain):
    whole_rows = lax.all_gather(hidden, "tensor", axis=1, tiled=True)
    wide_rows = whole_rows.astype(jnp.float32)
    pre_scale = lax.rsqrt(
        jnp.sum(wide_rows * wide_rows, axis=1, keepdims=True) / pre_gain.shape[0] + NORM_EPS
    )
    normed = (wide_rows * pre_scale * pre_gain).astype(jnp.bfloat16)
    return (normed, pre_scale)


def attention_layer(hidden, normed, weights, adapters, lengths, post_local):
    w_query, w_key, value_projection, w_out, a_query, a_value = weights
    tok_rows, full_width = normed.shape
    seqs_here = lengths.shape[0]
    length = tok_rows // seqs_here
    query_rows = jnp.dot(normed, w_query, preferred_element_type=jnp.float32)
    keys_before_rotation = jnp.dot(normed, w_key, preferred_element_type=jnp.float32)
    value_rows = jnp.dot(normed, value_projection, preferred_element_type=jnp.float32)
    low_rank_update = None
    if adapters is not None:
        query_second_factor, value_second_factor = adapters
        rank_size = query_second_factor.shape[0]
        low_rank_update = jnp.dot(
            normed, jnp.concatenate([a_query, a_value], axis=1), preferred_element_type=jnp.float32
        ).astype(jnp.bfloat16)
        query_rows = query_rows + ADAPTER_SCALE * jnp.dot(
            low_rank_update[:, :rank_size], query_second_factor, preferred_element_type=jnp.float32
        )
        value_rows = value_rows + ADAPTER_SCALE * jnp.dot(
            low_rank_update[:, rank_size:], value_second_factor, preferred_element_type=jnp.float32
        )
    q_heads = query_rows.shape[1] // HEAD_SIZE
    kv_heads = keys_before_rotation.shape[1] // HEAD_SIZE
    query_rows = apply_rotation(
        query_rows.reshape(seqs_here, length, q_heads, HEAD_SIZE), 1.0
    ).astype(jnp.bfloat16)
    rotated_keys = apply_rotation(
        keys_before_rotation.reshape(seqs_here, length, kv_heads, HEAD_SIZE), 1.0
    ).astype(jnp.bfloat16)
    value_rows = value_rows.reshape(seqs_here, length, kv_heads, HEAD_SIZE).astype(jnp.bfloat16)
    mixed_out, probs_low, probabilities, capped = attend(
        query_rows, rotated_keys, value_rows, lengths
    )
    head_terms = lax.dot_general(
        mixed_out.reshape(tok_rows, q_heads * HEAD_SIZE),
        w_out,
        (((1,), (1,)), ((), ())),
        preferred_element_type=jnp.float32,
    )
    summed = lax.psum_scatter(
        head_terms.astype(jnp.bfloat16), "tensor", scatter_dimension=1, tiled=True
    ).astype(jnp.float32)
    squares = lax.psum(jnp.sum(summed * summed, axis=1), "tensor")
    post_scale = lax.rsqrt(squares[:, None] / full_width + NORM_EPS)
    result = hidden.astype(jnp.float32) + summed * post_scale * post_local
    saved = (
        low_rank_update,
        query_rows,
        rotated_keys,
        value_rows,
        probs_low,
        probabilities,
        capped,
        summed,
        post_scale,
    )
    return (result, saved)


def body(
    ref_hidden,
    pol_hidden,
    readout,
    lengths,
    pairing,
    pre_gain,
    post_gain,
    w_query,
    w_key,
    value_projection,
    w_out,
    a_query,
    a_value,
    query_second_factor,
    value_second_factor,
):
    tok_rows, part_width = pol_hidden.shape
    seqs_here = lengths.shape[0]
    length = tok_rows // seqs_here
    tensor_rank = lax.axis_index("tensor")
    data_rank = lax.axis_index("dp")
    all_seqs = seqs_here * lax.axis_size("dp")
    full_width = part_width * lax.axis_size("tensor")
    pre_local = lax.dynamic_slice_in_dim(pre_gain, tensor_rank * part_width, part_width)
    post_local = lax.dynamic_slice_in_dim(post_gain, tensor_rank * part_width, part_width)
    weights = (
        lax.all_gather(w_query, "dp", axis=0, tiled=True),
        lax.all_gather(w_key, "dp", axis=0, tiled=True),
        lax.all_gather(value_projection, "dp", axis=0, tiled=True),
        lax.all_gather(w_out, "dp", axis=0, tiled=True),
        lax.all_gather(a_query, "dp", axis=0, tiled=True),
        lax.all_gather(a_value, "dp", axis=0, tiled=True),
    )
    w_query_all, w_key_all, w_value_all, w_out_all, a_query_all, a_value_all = weights
    ref_normed, ref_scale = normalize(ref_hidden, pre_gain)
    ref_result, ref_saved = attention_layer(
        ref_hidden, ref_normed, weights, None, lengths, post_local
    )
    pol_normed, pol_scale = normalize(pol_hidden, pre_gain)
    pol_result, pol_saved = attention_layer(
        pol_hidden,
        pol_normed,
        weights,
        (query_second_factor, value_second_factor),
        lengths,
        post_local,
    )
    readout_wide = readout.astype(jnp.float32)
    living = (jnp.arange(length)[None, :] < lengths[:, None]).astype(jnp.float32)

    def sequence_score(result):
        return jnp.sum(
            jnp.sum(result * readout_wide, axis=1).reshape(seqs_here, length) * living, axis=1
        )

    placed = jnp.zeros((2, all_seqs), jnp.float32)
    offset = data_rank * seqs_here
    placed = lax.dynamic_update_slice(
        placed,
        jnp.stack([sequence_score(ref_result), sequence_score(pol_result)]),
        (jnp.int32(0), offset),
    )
    scores = lax.psum(placed, ("dp", "tensor"))
    ratios = scores[1] - scores[0]
    chooser = (pairing[:, None] == jnp.arange(all_seqs)[None, :]).astype(jnp.float32)
    picked = jnp.dot(chooser, ratios, precision=lax.Precision.HIGHEST).reshape(-1, 2)
    margins = DPO_BETA * (picked[:, 0] - picked[:, 1])
    dpo_loss = jnp.sum(jax.nn.softplus(-margins))
    pair_pull = DPO_BETA * LOSS_SCALE * jax.nn.sigmoid(-margins)
    signed = jnp.stack([-pair_pull, pair_pull], axis=1).reshape(-1)
    coefficients = jnp.dot(signed, chooser, precision=lax.Precision.HIGHEST)
    local_coef = lax.dynamic_slice_in_dim(coefficients, offset, seqs_here)
    grad_result = (local_coef[:, None] * living).reshape(tok_rows, 1) * readout_wide
    (
        low_rank_update,
        query_rows,
        rotated_keys,
        value_rows,
        probs_low,
        probabilities,
        capped,
        summed,
        post_scale,
    ) = pol_saved
    post_dot = lax.psum(jnp.sum(summed * post_local * grad_result, axis=1), "tensor")
    grad_summed = (
        post_scale * post_local * grad_result
        - summed * post_scale**3 * post_dot[:, None] / full_width
    )
    grad_wide = lax.all_gather(grad_summed.astype(jnp.bfloat16), "tensor", axis=1, tiled=True)
    grad_mixed = jnp.dot(grad_wide, w_out_all, preferred_element_type=jnp.float32).astype(
        jnp.bfloat16
    )
    q_heads = query_rows.shape[2]
    grad_q_rot, rotated_key_gradient, value_head_gradient = attend_back(
        grad_mixed.reshape(seqs_here, length, q_heads, HEAD_SIZE),
        query_rows,
        rotated_keys,
        value_rows,
        probs_low,
        probabilities,
        capped,
    )
    query_rows_gradient = (
        apply_rotation(grad_q_rot, -1.0).reshape(tok_rows, -1).astype(jnp.bfloat16)
    )
    key_rows_gradient = (
        apply_rotation(rotated_key_gradient, -1.0).reshape(tok_rows, -1).astype(jnp.bfloat16)
    )
    value_rows_gradient = value_head_gradient.reshape(tok_rows, -1).astype(jnp.bfloat16)
    rank_size = query_second_factor.shape[0]
    rows_contraction = (((0,), (0,)), ((), ()))
    contract_cols = (((1,), (1,)), ((), ()))
    query_adapter_term = ADAPTER_SCALE * lax.dot_general(
        low_rank_update[:, :rank_size],
        query_rows_gradient,
        rows_contraction,
        preferred_element_type=jnp.float32,
    )
    value_adapter_term = ADAPTER_SCALE * lax.dot_general(
        low_rank_update[:, rank_size:],
        value_rows_gradient,
        rows_contraction,
        preferred_element_type=jnp.float32,
    )
    query_factor_gradient, value_factor_gradient = (
        lax.psum(query_adapter_term.astype(jnp.bfloat16), "dp").astype(jnp.float32),
        lax.psum(value_adapter_term.astype(jnp.bfloat16), "dp").astype(jnp.float32),
    )
    adapter_grad = jnp.concatenate(
        [
            ADAPTER_SCALE
            * lax.dot_general(
                query_rows_gradient,
                query_second_factor,
                contract_cols,
                preferred_element_type=jnp.float32,
            ),
            ADAPTER_SCALE
            * lax.dot_general(
                value_rows_gradient,
                value_second_factor,
                contract_cols,
                preferred_element_type=jnp.float32,
            ),
        ],
        axis=1,
    ).astype(jnp.bfloat16)
    adapter_term = lax.dot_general(
        pol_normed, adapter_grad, rows_contraction, preferred_element_type=jnp.float32
    )
    adapter_part = lax.psum_scatter(
        adapter_term.astype(jnp.bfloat16), "dp", scatter_dimension=0, tiled=True
    )
    grad_a = lax.psum(adapter_part, "tensor").astype(jnp.float32)
    a_both = jnp.concatenate([a_query_all, a_value_all], axis=1)
    input_terms = lax.dot_general(
        query_rows_gradient, w_query_all, contract_cols, preferred_element_type=jnp.float32
    )
    input_terms = input_terms + lax.dot_general(
        key_rows_gradient, w_key_all, contract_cols, preferred_element_type=jnp.float32
    )
    input_terms = input_terms + lax.dot_general(
        value_rows_gradient, w_value_all, contract_cols, preferred_element_type=jnp.float32
    )
    input_terms = input_terms + lax.dot_general(
        adapter_grad, a_both, contract_cols, preferred_element_type=jnp.float32
    )
    input_whole = lax.psum(input_terms.astype(jnp.bfloat16), "tensor").astype(jnp.float32)
    grad_normed = lax.dynamic_slice_in_dim(input_whole, tensor_rank * part_width, part_width, 1)
    narrow = pol_hidden.astype(jnp.float32)
    pre_dot = lax.psum(jnp.sum(narrow * pre_local * grad_normed, axis=1), "tensor")
    grad_hidden = (
        grad_result
        + pol_scale * pre_local * grad_normed
        - narrow * pol_scale**3 * pre_dot[:, None] / full_width
    )
    return (
        pol_result.astype(jnp.bfloat16),
        ref_result.astype(jnp.bfloat16),
        dpo_loss,
        grad_hidden.astype(jnp.bfloat16),
        grad_a,
        query_factor_gradient,
        value_factor_gradient,
    )


def solution(mesh):
    placed = (
        P("dp", "tensor"),
        P("dp", "tensor"),
        P("dp", "tensor"),
        P("dp"),
        P(),
        P(),
        P(),
        P("dp", "tensor"),
        P("dp", "tensor"),
        P("dp", "tensor"),
        P("dp", "tensor"),
        P("dp", None),
        P("dp", None),
        P(None, "tensor"),
        P(None, "tensor"),
    )
    return jax.shard_map(
        body,
        mesh=mesh,
        in_specs=placed,
        out_specs=(
            P("dp", "tensor"),
            P("dp", "tensor"),
            P(),
            P("dp", "tensor"),
            P("dp", None),
            P(None, "tensor"),
            P(None, "tensor"),
        ),
        check_vma=False,
    )
```

profile of v0, /device:TPU:0, one launch (start us, length us, event | category | flops | bytes accessed | tf_op | source)
XLA Modules:
  0.0 823.5 jit_solution(8016594998505936199)
XLA Ops:
  11.2 9.0 %all_gather.29 = bf16[4608,64]{0,1:T(8,128)(2,1)S(1)} all-gather(bf16[1152,64]{0,1:T(8,128)(2,1)S(1)} %copy-done.29), channel_id=1, replica_groups=mesh['dp'=4,'tensor'=8] {'dp'}, dimensions={0}, use_global_device_ids=true | all-gather | bytes 737280 | tf_op jit(solution)/shard_map/all_gather | solution.py:194
  20.3 7.6 all_gather.30
  29.8 41.2 %all-gather.21.cloned.1.call-done = bf16[8,576,288]{1,2,0:T(8,128)(2,1)} async-done(((bf16[1,576,288]{1,2,0:T(8,128)(2,1)}), bf16[8,576,288]{1,2,0:T(8,128)(2,1)}) %all-gather.21.cloned.1.call-update) | async-done | bytes 2654224 | tf_op jit(solution)/shard_map/all_gather | solution.py:95
  71.0 5.3 copy.72
  76.4 7.2 reshape.270
  83.6 46.3 %all-gather.19.cloned.1.call-done = bf16[8,576,288]{1,2,0:T(8,128)(2,1)} async-done(((bf16[1,576,288]{1,2,0:T(8,128)(2,1)}), bf16[8,576,288]{1,2,0:T(8,128)(2,1)}) %all-gather.19.cloned.1.call-update) | async-done | bytes 2654224 | tf_op jit(solution)/shard_map/all_gather | solution.py:95
  129.8 5.3 copy.64
  135.2 7.8 reshape.269
  143.0 3.1 multiply_reduce_fusion
  149.6 3.3 multiply_convert_fusion
  154.1 3.3 fusion.141
  157.6 3.2 fusion.139
  162.0 17.6 %all-gather.11.cloned.1.call-done = bf16[4608,256]{1,0:T(8,128)(2,1)} async-done(((bf16[1152,256]{1,0:T(8,128)(2,1)}), bf16[4608,256]{1,0:T(8,128)(2,1)}) %all-gather.11.cloned.1.call-update) | async-done | bytes 2359312 | tf_op jit(solution)/shard_map/all_gather | solution.py:192
  179.6 3.3 convolution_convert_fusion.6
  186.1 32.4 %all-gather.15.cloned.1.call-done = bf16[4608,512]{1,0:T(8,128)(2,1)} async-done(((bf16[1152,512]{1,0:T(8,128)(2,1)}), bf16[4608,512]{1,0:T(8,128)(2,1)}) %all-gather.15.cloned.1.call-update) | async-done | bytes 4718608 | tf_op jit(solution)/shard_map/all_gather | solution.py:190
  218.5 5.5 fusion.142
  225.2 4.4 fusion.140
  230.7 2.1 reshape.256
  232.8 2.9 subtract_convert_fusion.1
  239.0 18.4 %all-gather.17.cloned.1.call-done = bf16[4608,512]{1,0:T(8,128)(2,1)} async-done(((bf16[1152,512]{1,0:T(8,128)(2,1)}), bf16[4608,512]{1,0:T(8,128)(2,1)}) %all-gather.17.cloned.1.call-update) | async-done | bytes 4718608 | tf_op jit(solution)/shard_map/all_gather | solution.py:193
  257.4 5.4 convolution_convert_fusion
  262.8 4.7 copy.110
  267.8 2.5 fusion.138
  276.2 5.6 convolution_convert_fusion.1
  281.8 4.7 copy.108
  288.0 59.2 %reduce-scatter.12.cloned.1.call-done = bf16[576,288]{1,0:T(8,128)(2,1)} async-done(((bf16[4608,288]{1,0:T(8,128)(2,1)}), bf16[576,288]{1,0:T(8,128)(2,1)}) %reduce-scatter.12.cloned.1.call-update) | async-done | bytes 331792
  349.1 80.8 %reduce-scatter.10.cloned.1.call-done = bf16[576,288]{1,0:T(8,128)(2,1)} async-done(((bf16[4608,288]{1,0:T(8,128)(2,1)}), bf16[576,288]{1,0:T(8,128)(2,1)}) %reduce-scatter.10.cloned.1.call-update) | async-done | bytes 331792
  432.4 20.1 %all-reduce = (f32[288]{0:T(512)S(1)}, f32[288]{0:T(512)S(1)}) all-reduce(f32[288]{0:T(512)S(1)} %fusion.45, f32[288]{0:T(512)S(1)} %fusion.32), channel_id=1, replica_groups=mesh['dp'=4,'tensor'=8] {'tensor'}, use_global_device_ids=true, to_apply=%region_4.5 | all-reduce | flops 576 | bytes 4608 | tf_op jit(solution)/shard_map/psum | solution.py:146
  452.5 2.6 fusion.43
  457.0 36.8 %psum.65 = f32[2,12]{1,0:T(2,128)S(1)} all-reduce(f32[2,12]{1,0:T(2,128)S(1)} %dynamic_update_slice.3), channel_id=1, replica_groups=mesh['dp'=4,'tensor'=8] {'dp','tensor'}, use_global_device_ids=true, to_apply=%region_14.15 | all-reduce | flops 24 | bytes 192 | tf_op jit(solution)/shard_map/psum | solution.py:226
  496.8 21.1 %psum.66 = f32[288]{0:T(512)S(1)} all-reduce(f32[288]{0:T(512)S(1)} %fusion.38), channel_id=1, replica_groups=mesh['dp'=4,'tensor'=8] {'tensor'}, use_global_device_ids=true, to_apply=%region_17.18 | all-reduce | flops 288 | bytes 2304 | tf_op jit(solution)/shard_map/psum | solution.py:248
  519.2 55.1 %all-gather.23.cloned.1.call-done = bf16[8,576,288]{1,2,0:T(8,128)(2,1)} async-done(((bf16[1,576,288]{1,2,0:T(8,128)(2,1)}), bf16[8,576,288]{1,2,0:T(8,128)(2,1)}) %all-gather.23.cloned.1.call-update) | async-done | bytes 2654224 | tf_op jit(solution)/shard_map/all_gather | solution.py:253
  574.4 4.4 copy.82
  578.8 5.6 reshape.268
  584.4 5.4 convolution_convert_fusion.3
  590.9 2.1 convolution_bitcast_fusion
  592.9 2.0 fusion.19
  595.0 3.3 fusion.27
  602.9 2.2 convolution_convert_fusion.2
  605.2 2.5 convolution_bitcast_fusion.2
  609.0 4.3 fusion.58
  616.3 2.4 fusion.1
  618.7 10.8 %reduce-scatter.8.cloned.1.call-done = bf16[1152,128]{1,0:T(8,128)(2,1)} async-done(((bf16[4608,128]{1,0:T(8,128)(2,1)}), bf16[1152,128]{1,0:T(8,128)(2,1)}) %reduce-scatter.8.cloned.1.call-update) | async-done | bytes 294928 | tf_op jit(solution)/shard_map/reduce_scatter | solution.py:315
  631.2 10.5 %psum.71 = bf16[64,256]{1,0:T(8,128)(2,1)S(1)} all-reduce(bf16[64,256]{1,0:T(8,128)(2,1)S(1)} %fusion.23), channel_id=1, replica_groups=mesh['dp'=4,'tensor'=8] {'dp'}, use_global_device_ids=true, to_apply=%region_25.26 | all-reduce | flops 16384 | bytes 65536 | tf_op jit(solution)/shard_map/psum | solution.py:291
  642.4 21.6 %all-reduce.5.cloned.1.call-done = bf16[64,512]{1,0:T(8,128)(2,1)} async-done(((bf16[64,512]{1,0:T(8,128)(2,1)}), bf16[64,512]{1,0:T(8,128)(2,1)}) %all-reduce.5.cloned.1.call-update) | async-done | bytes 65552 | tf_op jit(solution)/shard_map/psum | solution.py:290
  665.5 126.0 %all-reduce.7.cloned.1.call-done = (bf16[288,4608]{1,0:T(8,128)(2,1)}, bf16[1152,128]{1,0:T(8,128)(2,1)}) async-done(((bf16[288,4608]{1,0:T(8,128)(2,1)}, bf16[1152,128]{1,0:T(8,128)(2,1)}), (bf16[288,4608]{1,0:T(8,128)(2,1)}, bf16[1152,128]{1,0:T(8,128)(2,1)})) %all-reduce.7.cloned.1.call-update) | async-done | bytes 2949136 | tf_op jit(solution)/shard_map/psum | solution.py:332
  792.8 19.4 %psum.68 = f32[288]{0:T(512)S(1)} all-reduce(f32[288]{0:T(512)S(1)} %fusion.35), channel_id=1, replica_groups=mesh['dp'=4,'tensor'=8] {'tensor'}, use_global_device_ids=true, to_apply=%region_21.22 | all-reduce | flops 288 | bytes 2304 | tf_op jit(solution)/shard_map/psum | solution.py:335
  814.1 2.4 fusion.40
  (195 shorter events, 55.5 us)
Async XLA Ops:
  7.2 222.5 %copy-start = (bf16[64,512]{1,0:T(8,128)(2,1)S(1)}, bf16[64,512]{1,0:T(8,128)(2,1)}, u32[]{:S(2)}) copy-start(bf16[64,512]{1,0:T(8,128)(2,1)} %param.28) | copy-start | bytes 196612
  7.2 4.1 copy-start.29
  7.2 63.8 %all-gather.21.cloned.1.call-start = ((), (), s32[]{:S(2)}) async-start(), calls=%async_computation.10 | async-start | bytes 3317760 | tf_op jit(solution)/shard_map/all_gather | solution.py:95
  7.9 121.9 %all-gather.19.cloned.1.call-start = ((), (), s32[]{:S(2)}) async-start(), calls=%async_computation.9 | async-start | bytes 3317760 | tf_op jit(solution)/shard_map/all_gather | solution.py:95
  8.7 11.6 %copy-start.30 = (bf16[1152,64]{0,1:T(8,128)(2,1)S(1)}, bf16[1152,64]{0,1:T(8,128)(2,1)}, u32[]{:S(2)}) copy-start(bf16[1152,64]{0,1:T(8,128)(2,1)} %param.27) | copy-start | bytes 442372
  8.7 145.4 %all-gather.13.cloned.1.call-start = ((), (), s32[]{:S(2)}) async-start(), calls=%async_computation.4 | async-start | bytes 2949120 | tf_op jit(solution)/shard_map/all_gather | solution.py:191
  9.4 170.2 %all-gather.11.cloned.1.call-start = ((), (), s32[]{:S(2)}) async-start(), calls=%async_computation.3 | async-start | bytes 2949120 | tf_op jit(solution)/shard_map/all_gather | solution.py:192
  10.0 18.0 %copy-start.40 = (s32[3]{0:T(128)S(1)}, s32[3]{0:T(128)}, u32[]{:S(2)}) copy-start(s32[3]{0:T(128)} %param.18) | copy-start | bytes 40
  10.0 208.5 %all-gather.15.cloned.1.call-start = ((), (), s32[]{:S(2)}) async-start(), calls=%async_computation.5 | async-start | bytes 5898240 | tf_op jit(solution)/shard_map/all_gather | solution.py:190
  10.6 246.8 %all-gather.17.cloned.1.call-start = ((), (), s32[]{:S(2)}) async-start(), calls=%async_computation.6 | async-start | bytes 5898240 | tf_op jit(solution)/shard_map/all_gather | solution.py:193
  11.2 336.0 %reduce-scatter.12.cloned.1.call-start = ((), (), s32[]{:S(2)}) async-start(), calls=%async_computation.13 | async-start | bytes 3981312
  28.1 48.3 %copy-start.3 = (bf16[4608,128]{0,1:T(8,128)(2,1)}, bf16[4608,128]{0,1:T(8,128)(2,1)S(1)}, u32[]{:S(2)}) copy-start(bf16[4608,128]{0,1:T(8,128)(2,1)S(1)} %constant_dynamic-update-slice_fusion) | copy-start | bytes 3538948
  29.8 203.0 %copy-start.12 = (f32[96,64]{1,0:T(8,128)}, f32[96,64]{1,0:T(8,128)S(1)}, u32[]{:S(2)}) copy-start(f32[96,64]{1,0:T(8,128)S(1)} %get-tuple-element.50) | copy-start | bytes 73732
  135.2 12.9 %copy-start.36 = (f32[4608]{0:T(1024)S(1)}, f32[4608]{0:T(1024)}, u32[]{:S(2)}) copy-start(f32[4608]{0:T(1024)} %param.20) | copy-start | bytes 55300
  143.0 4.1 copy-start.2
  147.1 2.5 copy-start.1
  148.1 4.9 copy-start.37
  183.6 1.6 copy-start.4
  232.7 3.0 copy-start.25
  232.7 3.0 copy-start.26
  232.8 3.0 copy-start.31
  267.6 2.8 copy-start.34
  267.6 4.6 copy-start.15
  267.6 4.7 copy-start.14
  267.6 162.2 %reduce-scatter.10.cloned.1.call-start = ((), (), s32[]{:S(2)}) async-start(), calls=%async_computation.12 | async-start | bytes 3981312
  272.2 2.9 copy-start.16
  272.2 2.6 copy-start.32
  272.3 1.7 copy-start.19
  272.3 3.9 copy-start.20
  286.5 166.0 %copy-start.6 = (bf16[288,576]{1,0:T(8,128)(2,1)S(1)}, bf16[288,576]{1,0:T(8,128)(2,1)}, u32[]{:S(2)}) copy-start(bf16[288,576]{1,0:T(8,128)(2,1)} %param.17) | copy-start | bytes 995332
  286.5 287.9 %all-gather.23.cloned.1.call-start = ((), (), s32[]{:S(2)}) async-start(), calls=%async_computation.11 | async-start | bytes 3317760 | tf_op jit(solution)/shard_map/all_gather | solution.py:253
  519.0 110.6 %reduce-scatter.8.cloned.1.call-start = ((), (), s32[]{:S(2)}) async-start(), calls=%async_computation.7 | async-start | bytes 1474560 | tf_op jit(solution)/shard_map/reduce_scatter | solution.py:315
  584.4 8.5 %copy-start.33 = (pred[3,96,96]{1,2,0:T(8,128)(4,1)S(1)}, pred[3,96,96]{1,2,0:T(8,128)(4,1)}, u32[]{:S(2)}) copy-start(pred[3,96,96]{1,2,0:T(8,128)(4,1)} %broadcast_and_fusion) | copy-start | bytes 82948
  584.4 8.5 %copy-start.45 = (f32[3,2,2,96]{3,2,1,0:T(2,128)S(1)}, f32[3,2,2,96]{3,2,1,0:T(2,128)}, u32[]{:S(2)}) copy-start(f32[3,2,2,96]{3,2,1,0:T(2,128)} %copy-done.44) | copy-start | bytes 13828
  595.0 4.8 copy-start.28
  595.0 5.6 copy-start.35
  595.0 5.8 copy-start.13
  595.0 5.8 copy-start.17
  605.1 2.6 copy-start.18
  605.1 58.9 %all-reduce.5.cloned.1.call-start = ((), (), s32[]{:S(2)}) async-start(), calls=%async_computation.8 | async-start | bytes 131072 | tf_op jit(solution)/shard_map/psum | solution.py:290
  609.0 4.3 copy-start.8
  609.0 182.5 %all-reduce.7.cloned.1.call-start = ((), (), s32[]{:S(2)}) async-start(), calls=%async_computation.14 | async-start | bytes 5898240 | tf_op jit(solution)/shard_map/psum | solution.py:332
  613.3 1.7 copy-start.9
  613.3 1.7 copy-start.11
  618.7 11.6 %copy-start.42 = (f32[6,1]{0,1:T(1,128)S(1)}, f32[6,1]{0,1:T(1,128)}, u32[]{:S(2)}) copy-start(f32[6,1]{0,1:T(1,128)} %get-tuple-element.17) | copy-start | bytes 76
  618.7 172.8 %copy-start.7 = (bf16[288,576]{1,0:T(8,128)(2,1)S(1)}, bf16[288,576]{1,0:T(8,128)(2,1)}, u32[]{:S(2)}) copy-start(bf16[288,576]{1,0:T(8,128)(2,1)} %param.16) | copy-start | bytes 995332
  618.7 195.4 %copy-start.38 = (f32[288]{0:T(512)S(1)}, f32[288]{0:T(512)}, u32[]{:S(2)}) copy-start(f32[288]{0:T(512)} %copy-done.37) | copy-start | bytes 3460
  618.7 195.4 %copy-start.39 = (f32[288]{0:T(512)S(1)}, f32[288]{0:T(512)}, u32[]{:S(2)}) copy-start(f32[288]{0:T(512)} %get-tuple-element.44) | copy-start | bytes 3460
  (10 other events, 10.3 us)
Sparse Core Ops, SparseCore 0:
  10.2 60.8 all-gather.20
  73.2 56.5 all-gather.18
  131.4 22.6 all-gather.12
  155.5 24.0 all-gather.10
  181.0 37.4 all-gather.14
  219.9 37.4 all-gather.16
  267.7 79.4 reduce-scatter.11
  350.8 79.0 reduce-scatter.9
  519.1 55.2 all-gather.22
  605.2 24.2 reduce-scatter.7
  632.4 31.5 all-reduce.4
  667.5 123.9 all-reduce.6
where the time goes:
time: 829 us; the launch traced here: 824 us
  waiting for transfers between devices  514 us (62%)
  blocking collectives  125 us (15%)
  matrix products  69.4 us (8%)
  local copies, waits for them, and re-layouts  68.9 us (8%)
  other arithmetic  30.4 us (4%)
  between operations  15.1 us (2%)
    unnamed x14, waiting for transfers between devices  144 us
    psum x1, waiting for transfers between devices, body(): lax.psum(input_terms.astype(jnp.bfloat16), 'tensor').astype(jnp.float32)  126 us
    all_gather x2, waiting for transfers between devices, normalize(): whole_rows = lax.all_gather(hidden, 'tensor', axis=1, tiled=True)  87.5 us
    all_gather x1, waiting for transfers between devices, body(): lax.all_gather(grad_summed.astype(jnp.bfloat16), 'tensor', axis=1, tiled=...  55.1 us
    psum x1, blocking collectives, body(): scores = lax.psum(placed, ('dp', 'tensor'))  36.8 us
    all_gather x1, waiting for transfers between devices, body(): lax.all_gather(w_query, 'dp', axis=0, tiled=True)  32.4 us
    convert_element_type x4, local copies, waits for them, and re-layouts, normalize(): wide_rows = whole_rows.astype(jnp.float32)  25.6 us
    unnamed x98, local copies, waits for them, and re-layouts  24.7 us
  transfers between devices with their start and end apart: 12, of which 12 were waited for; matrix products, arithmetic and copies ran while one was open for 13% of the time, Pallas kernels for 0%

commit v1 on v0

--- a/solution.py
+++ b/solution.py
@@ -92,7 +92,14 @@
 
 
 def normalize(hidden, pre_gain):
-    whole_rows = lax.all_gather(hidden, "tensor", axis=1, tiled=True)
+    ring = [hidden]
+    for hop in range(7):
+        ring.append(lax.ppermute(ring[-1], "tensor", [(dev, (dev + 1) % 8) for dev in range(8)]))
+    whole_rows = jnp.roll(
+        jnp.concatenate(ring[::-1], axis=1),
+        (lax.axis_index("tensor") + 1) * ring[0].shape[1],
+        axis=1,
+    )
     wide_rows = whole_rows.astype(jnp.float32)
     pre_scale = lax.rsqrt(
         jnp.sum(wide_rows * wide_rows, axis=1, keepdims=True) / pre_gain.shape[0] + NORM_EPS

time: 829 us -> 751 us (0.906)
  waiting for transfers between devices: 514 us -> 439 us
  local copies, waits for them, and re-layouts: 68.9 us -> 52.3 us
    all_gather x2 -> x0, waiting for transfers between devices: 87.5 us -> none  [normalize(): whole_rows = lax.all_gather(hidden, 'tensor', axis=1, tiled=True)]
    ppermute x0 -> x14, waiting for transfers between devices: none -> 86.5 us  [normalize(): lax.ppermute(ring[-1], 'tensor', [(dev, (dev + 1) % 8) for dev in range(8)])]
    all_gather x1, waiting for transfers between devices: 32.4 us -> 0.01 us  [body(): lax.all_gather(w_query, 'dp', axis=0, tiled=True)]
    convert_element_type x4 -> x0, local copies, waits for them, and re-layouts: 25.6 us -> none  [normalize(): wide_rows = whole_rows.astype(jnp.float32)]
    all_gather x1, waiting for transfers between devices: 18.4 us -> 0.01 us  [body(): lax.all_gather(w_out, 'dp', axis=0, tiled=True)]
    all_gather x1, waiting for transfers between devices: 17.6 us -> 0.02 us  [body(): lax.all_gather(value_projection, 'dp', axis=0, tiled=True)]
    concatenate x0 -> x2, local copies, waits for them, and re-layouts: none -> 9.44 us  [normalize(): jnp.concatenate(ring[::-1], axis=1)]
    unnamed x14 -> x12, waiting for transfers between devices: 144 us -> 139 us
  transfers between devices with their start and end apart: 12 -> 24, of which waited for: 12 -> 19; matrix products, arithmetic and copies ran while one was open for 13% -> 14% of each run, Pallas kernels for 0% -> 0%
where the time goes in v1:
time: 751 us; the launch traced here: 746 us
  waiting for transfers between devices  439 us (58%)
  blocking collectives  127 us (17%)
  matrix products  72 us (10%)
  local copies, waits for them, and re-layouts  52.3 us (7%)
  other arithmetic  34 us (5%)
  between operations  15.2 us (2%)
    unnamed x12, waiting for transfers between devices  139 us
    psum x1, waiting for transfers between devices, body(): lax.psum(input_terms.astype(jnp.bfloat16), 'tensor').astype(jnp.float32)  126 us
    ppermute x14, waiting for transfers between devices, normalize(): lax.ppermute(ring[-1], 'tensor', [(dev, (dev + 1) % 8) for dev in range(8)])  86.5 us
    all_gather x1, waiting for transfers between devices, body(): lax.all_gather(grad_summed.astype(jnp.bfloat16), 'tensor', axis=1, tiled=...  55.1 us
    psum x1, blocking collectives, body(): scores = lax.psum(placed, ('dp', 'tensor'))  36.8 us
    unnamed x116, local copies, waits for them, and re-layouts  22.9 us
    psum x1, waiting for transfers between devices, body(): lax.psum(query_adapter_term.astype(jnp.bfloat16), 'dp').astype(jnp.float32)  21.6 us
    psum x1, blocking collectives, body(): lax.psum(jnp.sum(summed * post_local * grad_result, axis=1), 'tensor')  21.1 us
  transfers between devices with their start and end apart: 24, of which 19 were waited for; matrix products, arithmetic and copies ran while one was open for 14% of the time, Pallas kernels for 0%

profile of v1, /device:TPU:0, one launch (start us, length us, event | category | flops | bytes accessed | tf_op | source)
XLA Modules:
  0.0 745.9 jit_solution(11917479473526976985)
XLA Ops:
  9.5 3.0 collective-permute-start.7
  14.1 11.1 %collective-permute-done.7 = bf16[288,576]{1,0:T(8,128)(2,1)S(1)} collective-permute-done((bf16[288,576]{1,0:T(8,128)(2,1)}, bf16[288,576]{1,0:T(8,128)(2,1)S(1)}, u32[]{:S(2)}, u32[]{:S(2)}) %collective-permute-start.7) | collective-permute-done | bytes 331808 | tf_op jit(solution)/shard_map/ppermute | solution.py:97
  25.2 7.9 %collective-permute-done = bf16[288,576]{1,0:T(8,128)(2,1)S(1)} collective-permute-done((bf16[288,576]{1,0:T(8,128)(2,1)}, bf16[288,576]{1,0:T(8,128)(2,1)S(1)}, u32[]{:S(2)}, u32[]{:S(2)}) %collective-permute-start) | collective-permute-done | bytes 331808 | tf_op jit(solution)/shard_map/ppermute | solution.py:97
  33.9 7.1 collective-permute-done.8
  41.0 7.9 %collective-permute-done.1 = bf16[288,576]{1,0:T(8,128)(2,1)S(1)} collective-permute-done((bf16[288,576]{1,0:T(8,128)(2,1)S(1)}, bf16[288,576]{1,0:T(8,128)(2,1)S(1)}, u32[]{:S(2)}, u32[]{:S(2)}) %collective-permute-start.1) | collective-permute-done | bytes 331808 | tf_op jit(solution)/shard_map/ppermute | solution.py:97
  49.0 11.3 %all_gather.22 = bf16[4608,64]{0,1:T(8,128)(2,1)S(1)} all-gather(bf16[1152,64]{0,1:T(8,128)(2,1)S(1)} %copy-done.41), channel_id=1, replica_groups=mesh['dp'=4,'tensor'=8] {'dp'}, dimensions={0}, use_global_device_ids=true | all-gather | bytes 737280 | tf_op jit(solution)/shard_map/all_gather | solution.py:201
  64.8 7.5 %all_gather.23 = bf16[4608,64]{0,1:T(8,128)(2,1)S(1)} all-gather(bf16[1152,64]{0,1:T(8,128)(2,1)S(1)} %copy-done.42), channel_id=1, replica_groups=mesh['dp'=4,'tensor'=8] {'dp'}, dimensions={0}, use_global_device_ids=true | all-gather | bytes 737280 | tf_op jit(solution)/shard_map/all_gather | solution.py:202
  74.4 7.9 %collective-permute-done.3 = bf16[288,576]{1,0:T(8,128)(2,1)S(1)} collective-permute-done((bf16[288,576]{1,0:T(8,128)(2,1)S(1)}, bf16[288,576]{1,0:T(8,128)(2,1)S(1)}, u32[]{:S(2)}, u32[]{:S(2)}) %collective-permute-start.3) | collective-permute-done | bytes 331808 | tf_op jit(solution)/shard_map/ppermute | solution.py:97
  83.4 6.9 collective-permute-done.11
  90.2 7.9 %collective-permute-done.4 = bf16[288,576]{1,0:T(8,128)(2,1)S(1)} collective-permute-done((bf16[288,576]{1,0:T(8,128)(2,1)S(1)}, bf16[288,576]{1,0:T(8,128)(2,1)S(1)}, u32[]{:S(2)}, u32[]{:S(2)}) %collective-permute-start.4) | collective-permute-done | bytes 331808 | tf_op jit(solution)/shard_map/ppermute | solution.py:97
  98.9 7.1 collective-permute-done.12
  106.0 8.0 %collective-permute-done.5 = bf16[288,576]{1,0:T(8,128)(2,1)} collective-permute-done((bf16[288,576]{1,0:T(8,128)(2,1)S(1)}, bf16[288,576]{1,0:T(8,128)(2,1)}, u32[]{:S(2)}, u32[]{:S(2)}) %collective-permute-start.5) | collective-permute-done | bytes 331808 | tf_op jit(solution)/shard_map/ppermute | solution.py:97
  115.3 6.7 collective-permute-done.13
  122.0 3.9 concatenate.57
  125.9 3.6 collective-permute-done.6
  129.5 5.5 concatenate.51
  135.0 2.8 fusion.5
  137.9 2.7 fusion.2
  141.2 7.0 fusion.7
  152.3 3.3 fusion.145
  155.8 3.2 fusion.144
  160.2 3.2 fusion.23
  166.0 5.5 fusion.146
  172.7 4.8 convolution_add_fusion.3
  179.6 2.9 subtract_convert_fusion.1
  185.4 5.5 convolution_convert_fusion.1
  190.9 4.8 copy.104
  196.0 4.0 convolution_convert_fusion.6
  205.9 5.5 convolution_convert_fusion
  211.4 4.7 copy.106
  217.6 56.1 %reduce-scatter.10.cloned.1.call-done = bf16[576,288]{1,0:T(8,128)(2,1)} async-done(((bf16[4608,288]{1,0:T(8,128)(2,1)}), bf16[576,288]{1,0:T(8,128)(2,1)}) %reduce-scatter.10.cloned.1.call-update) | async-done | bytes 331792
  275.1 81.2 %reduce-scatter.12.cloned.1.call-done = bf16[576,288]{1,0:T(8,128)(2,1)} async-done(((bf16[4608,288]{1,0:T(8,128)(2,1)}), bf16[576,288]{1,0:T(8,128)(2,1)}) %reduce-scatter.12.cloned.1.call-update) | async-done | bytes 331792
  359.4 20.0 %all-reduce = (f32[288]{0:T(512)S(1)}, f32[288]{0:T(512)S(1)}) all-reduce(f32[288]{0:T(512)S(1)} %fusion.51, f32[288]{0:T(512)S(1)} %fusion.38), channel_id=1, replica_groups=mesh['dp'=4,'tensor'=8] {'tensor'}, use_global_device_ids=true, to_apply=%region_4.6 | all-reduce | flops 576 | bytes 4608 | tf_op jit(solution)/shard_map/psum | solution.py:153
  379.4 2.6 fusion.49
  382.7 36.8 %psum.65 = f32[2,12]{1,0:T(2,128)S(1)} all-reduce(f32[2,12]{1,0:T(2,128)S(1)} %dynamic_update_slice.3), channel_id=1, replica_groups=mesh['dp'=4,'tensor'=8] {'dp','tensor'}, use_global_device_ids=true, to_apply=%region_14.16 | all-reduce | flops 24 | bytes 192 | tf_op jit(solution)/shard_map/psum | solution.py:233
  420.7 21.1 %psum.66 = f32[288]{0:T(512)S(1)} all-reduce(f32[288]{0:T(512)S(1)} %fusion.44), channel_id=1, replica_groups=mesh['dp'=4,'tensor'=8] {'tensor'}, use_global_device_ids=true, to_apply=%region_17.19 | all-reduce | flops 288 | bytes 2304 | tf_op jit(solution)/shard_map/psum | solution.py:255
  443.1 55.1 %all-gather.15.cloned.1.call-done = bf16[8,576,288]{1,2,0:T(8,128)(2,1)} async-done(((bf16[1,576,288]{1,2,0:T(8,128)(2,1)}), bf16[8,576,288]{1,2,0:T(8,128)(2,1)}) %all-gather.15.cloned.1.call-update) | async-done | bytes 2654224 | tf_op jit(solution)/shard_map/all_gather | solution.py:260
  498.3 4.4 copy.78
  502.7 5.6 reshape.264
  508.3 5.4 convolution_convert_fusion.3
  518.3 3.3 fusion.33
  531.4 4.3 fusion.64
  538.3 3.7 fusion.1
  542.0 9.9 %reduce-scatter.8.cloned.1.call-done = bf16[1152,128]{1,0:T(8,128)(2,1)} async-done(((bf16[4608,128]{1,0:T(8,128)(2,1)}), bf16[1152,128]{1,0:T(8,128)(2,1)}) %reduce-scatter.8.cloned.1.call-update) | async-done | bytes 294928 | tf_op jit(solution)/shard_map/reduce_scatter | solution.py:322
  553.6 10.5 %psum.71 = bf16[64,256]{1,0:T(8,128)(2,1)S(1)} all-reduce(bf16[64,256]{1,0:T(8,128)(2,1)S(1)} %fusion.29), channel_id=1, replica_groups=mesh['dp'=4,'tensor'=8] {'dp'}, use_global_device_ids=true, to_apply=%region_25.27 | all-reduce | flops 16384 | bytes 65536 | tf_op jit(solution)/shard_map/psum | solution.py:298
  564.8 21.6 %all-reduce.5.cloned.1.call-done = bf16[64,512]{1,0:T(8,128)(2,1)} async-done(((bf16[64,512]{1,0:T(8,128)(2,1)}), bf16[64,512]{1,0:T(8,128)(2,1)}) %all-reduce.5.cloned.1.call-update) | async-done | bytes 65552 | tf_op jit(solution)/shard_map/psum | solution.py:297
  587.9 126.0 %all-reduce.7.cloned.1.call-done = (bf16[288,4608]{1,0:T(8,128)(2,1)}, bf16[1152,128]{1,0:T(8,128)(2,1)}) async-done(((bf16[288,4608]{1,0:T(8,128)(2,1)}, bf16[1152,128]{1,0:T(8,128)(2,1)}), (bf16[288,4608]{1,0:T(8,128)(2,1)}, bf16[1152,128]{1,0:T(8,128)(2,1)})) %all-reduce.7.cloned.1.call-update) | async-done | bytes 2949136 | tf_op jit(solution)/shard_map/psum | solution.py:339
  715.3 19.4 %psum.68 = f32[288]{0:T(512)S(1)} all-reduce(f32[288]{0:T(512)S(1)} %fusion.41), channel_id=1, replica_groups=mesh['dp'=4,'tensor'=8] {'tensor'}, use_global_device_ids=true, to_apply=%region_21.23 | all-reduce | flops 288 | bytes 2304 | tf_op jit(solution)/shard_map/psum | solution.py:342
  (233 shorter events, 70.3 us)
Async XLA Ops:
  7.2 144.1 %copy-start = (bf16[64,512]{1,0:T(8,128)(2,1)S(1)}, bf16[64,512]{1,0:T(8,128)(2,1)}, u32[]{:S(2)}) copy-start(bf16[64,512]{1,0:T(8,128)(2,1)} %param.30) | copy-start | bytes 196612
  7.2 41.8 %copy-start.41 = (bf16[1152,64]{0,1:T(8,128)(2,1)S(1)}, bf16[1152,64]{0,1:T(8,128)(2,1)}, u32[]{:S(2)}) copy-start(bf16[1152,64]{0,1:T(8,128)(2,1)} %param.28) | copy-start | bytes 442372
  7.2 57.6 %copy-start.42 = (bf16[1152,64]{0,1:T(8,128)(2,1)S(1)}, bf16[1152,64]{0,1:T(8,128)(2,1)}, u32[]{:S(2)}) copy-start(bf16[1152,64]{0,1:T(8,128)(2,1)} %param.29) | copy-start | bytes 442372
  7.2 145.1 %all-gather.9.cloned.1.call-start = ((), (), s32[]{:S(2)}) async-start(), calls=%async_computation.4 | async-start | bytes 2949120 | tf_op jit(solution)/shard_map/all_gather | solution.py:198
  7.9 152.2 %all-gather.7.cloned.1.call-start = ((), (), s32[]{:S(2)}) async-start(), calls=%async_computation.3 | async-start | bytes 2949120 | tf_op jit(solution)/shard_map/all_gather | solution.py:199
  8.7 157.3 %all-gather.11.cloned.1.call-start = ((), (), s32[]{:S(2)}) async-start(), calls=%async_computation.5 | async-start | bytes 5898240 | tf_op jit(solution)/shard_map/all_gather | solution.py:197
  9.4 73.9 %copy-start.51 = (s32[3]{0:T(128)S(1)}, s32[3]{0:T(128)}, u32[]{:S(2)}) copy-start(s32[3]{0:T(128)} %param.20) | copy-start | bytes 40
  9.4 112.5 %copy-start.11 = (bf16[288,576]{1,0:T(8,128)(2,1)S(1)}, bf16[288,576]{1,0:T(8,128)(2,1)}, u32[]{:S(2)}) copy-start(bf16[288,576]{1,0:T(8,128)(2,1)} %param.17) | copy-start | bytes 995332
  9.4 176.0 %all-gather.13.cloned.1.call-start = ((), (), s32[]{:S(2)}) async-start(), calls=%async_computation.6 | async-start | bytes 5898240 | tf_op jit(solution)/shard_map/all_gather | solution.py:200
  9.5 15.7 %collective-permute-start.7 = (bf16[288,576]{1,0:T(8,128)(2,1)}, bf16[288,576]{1,0:T(8,128)(2,1)S(1)}, u32[]{:S(2)}, u32[]{:S(2)}) collective-permute-start(bf16[288,576]{1,0:T(8,128)(2,1)} %param.17), channel_id=1, source_target_pairs={{0,1},{1,2},{2,3},{3,4},{4,5},{5,6},{6,7},{7,0},{8,9},{9,10},{10,1... | collective-permute-start | bytes 995336 | tf_op jit(solution)/shard_map/ppermute | solution.py:97
  12.5 20.6 %collective-permute-start = (bf16[288,576]{1,0:T(8,128)(2,1)}, bf16[288,576]{1,0:T(8,128)(2,1)S(1)}, u32[]{:S(2)}, u32[]{:S(2)}) collective-permute-start(bf16[288,576]{1,0:T(8,128)(2,1)} %param.18), channel_id=1, source_target_pairs={{0,1},{1,2},{2,3},{3,4},{4,5},{5,6},{6,7},{7,0},{8,9},{9,10},{10,1... | collective-permute-start | bytes 995336 | tf_op jit(solution)/shard_map/ppermute | solution.py:97
  25.2 23.7 %copy-start.22 = (bf16[288,576]{1,0:T(8,128)(2,1)}, bf16[288,576]{1,0:T(8,128)(2,1)S(1)}, u32[]{:S(2)}) copy-start(bf16[288,576]{1,0:T(8,128)(2,1)S(1)} %collective-permute-done.7) | copy-start | bytes 995332
  25.2 15.8 %collective-permute-start.8 = (bf16[288,576]{1,0:T(8,128)(2,1)S(1)}, bf16[288,576]{1,0:T(8,128)(2,1)S(1)}, u32[]{:S(2)}, u32[]{:S(2)}) collective-permute-start(bf16[288,576]{1,0:T(8,128)(2,1)S(1)} %collective-permute-done.7), channel_id=1, source_target_pairs={{0,1},{1,2},{2,3},{3,4},{4,5},{5,6},{6,7},{7,0},{8,9},{9,10},{10,1... | collective-permute-start | bytes 995336 | tf_op jit(solution)/shard_map/ppermute | solution.py:97
  33.8 15.1 %collective-permute-start.1 = (bf16[288,576]{1,0:T(8,128)(2,1)S(1)}, bf16[288,576]{1,0:T(8,128)(2,1)S(1)}, u32[]{:S(2)}, u32[]{:S(2)}) collective-permute-start(bf16[288,576]{1,0:T(8,128)(2,1)S(1)} %collective-permute-done), channel_id=1, source_target_pairs={{0,1},{1,2},{2,3},{3,4},{4,5},{5,6},{6,7},{7,0},{8,9},{9,10},{10,1... | collective-permute-start | bytes 995336 | tf_op jit(solution)/shard_map/ppermute | solution.py:97
  41.0 74.2 %copy-start.24 = (bf16[288,576]{1,0:T(8,128)(2,1)}, bf16[288,576]{1,0:T(8,128)(2,1)S(1)}, u32[]{:S(2)}) copy-start(bf16[288,576]{1,0:T(8,128)(2,1)S(1)} %collective-permute-done.8) | copy-start | bytes 995332
  41.0 19.3 %collective-permute-start.9 = (bf16[288,576]{1,0:T(8,128)(2,1)S(1)}, bf16[288,576]{1,0:T(8,128)(2,1)S(1)}, u32[]{:S(2)}, u32[]{:S(2)}) collective-permute-start(bf16[288,576]{1,0:T(8,128)(2,1)S(1)} %collective-permute-done.8), channel_id=1, source_target_pairs={{0,1},{1,2},{2,3},{3,4},{4,5},{5,6},{6,7},{7,0},{8,9},{9,10},{10,1... | collective-permute-start | bytes 995336 | tf_op jit(solution)/shard_map/ppermute | solution.py:97
  48.9 66.3 %copy-start.23 = (bf16[288,576]{1,0:T(8,128)(2,1)}, bf16[288,576]{1,0:T(8,128)(2,1)S(1)}, u32[]{:S(2)}) copy-start(bf16[288,576]{1,0:T(8,128)(2,1)S(1)} %collective-permute-done.1) | copy-start | bytes 995332
  48.9 14.9 %collective-permute-start.2 = (bf16[288,576]{1,0:T(8,128)(2,1)S(1)}, bf16[288,576]{1,0:T(8,128)(2,1)S(1)}, u32[]{:S(2)}, u32[]{:S(2)}) collective-permute-start(bf16[288,576]{1,0:T(8,128)(2,1)S(1)} %collective-permute-done.1), channel_id=1, source_target_pairs={{0,1},{1,2},{2,3},{3,4},{4,5},{5,6},{6,7},{7,0},{8,9},{9,10},{10,1... | collective-permute-start | bytes 995336 | tf_op jit(solution)/shard_map/ppermute | solution.py:97
  48.9 224.8 %reduce-scatter.10.cloned.1.call-start = ((), (), s32[]{:S(2)}) async-start(), calls=%async_computation.10 | async-start | bytes 3981312
  60.3 54.9 %copy-start.26 = (bf16[288,576]{1,0:T(8,128)(2,1)}, bf16[288,576]{1,0:T(8,128)(2,1)S(1)}, u32[]{:S(2)}) copy-start(bf16[288,576]{1,0:T(8,128)(2,1)S(1)} %collective-permute-done.9) | copy-start | bytes 995332
  60.3 14.2 %collective-permute-start.10 = (bf16[288,576]{1,0:T(8,128)(2,1)S(1)}, bf16[288,576]{1,0:T(8,128)(2,1)S(1)}, u32[]{:S(2)}, u32[]{:S(2)}) collective-permute-start(bf16[288,576]{1,0:T(8,128)(2,1)S(1)} %collective-permute-done.9), channel_id=1, source_target_pairs={{0,1},{1,2},{2,3},{3,4},{4,5},{5,6},{6,7},{7,0},{8,9},{9,10},{10,1... | collective-permute-start | bytes 995336 | tf_op jit(solution)/shard_map/ppermute | solution.py:97
  63.8 51.3 %copy-start.25 = (bf16[288,576]{1,0:T(8,128)(2,1)}, bf16[288,576]{1,0:T(8,128)(2,1)S(1)}, u32[]{:S(2)}) copy-start(bf16[288,576]{1,0:T(8,128)(2,1)S(1)} %collective-permute-done.2) | copy-start | bytes 995332
  63.9 18.5 %collective-permute-start.3 = (bf16[288,576]{1,0:T(8,128)(2,1)S(1)}, bf16[288,576]{1,0:T(8,128)(2,1)S(1)}, u32[]{:S(2)}, u32[]{:S(2)}) collective-permute-start(bf16[288,576]{1,0:T(8,128)(2,1)S(1)} %collective-permute-done.2), channel_id=1, source_target_pairs={{0,1},{1,2},{2,3},{3,4},{4,5},{5,6},{6,7},{7,0},{8,9},{9,10},{10,1... | collective-permute-start | bytes 995336 | tf_op jit(solution)/shard_map/ppermute | solution.py:97
  74.4 40.8 %copy-start.28 = (bf16[288,576]{1,0:T(8,128)(2,1)}, bf16[288,576]{1,0:T(8,128)(2,1)S(1)}, u32[]{:S(2)}) copy-start(bf16[288,576]{1,0:T(8,128)(2,1)S(1)} %collective-permute-done.10) | copy-start | bytes 995332
  74.4 15.8 %collective-permute-start.11 = (bf16[288,576]{1,0:T(8,128)(2,1)S(1)}, bf16[288,576]{1,0:T(8,128)(2,1)S(1)}, u32[]{:S(2)}, u32[]{:S(2)}) collective-permute-start(bf16[288,576]{1,0:T(8,128)(2,1)S(1)} %collective-permute-done.10), channel_id=1, source_target_pairs={{0,1},{1,2},{2,3},{3,4},{4,5},{5,6},{6,7},{7,0},{8,9},{9,10},{10,1... | collective-permute-start | bytes 995336 | tf_op jit(solution)/shard_map/ppermute | solution.py:97
  82.3 32.9 %copy-start.27 = (bf16[288,576]{1,0:T(8,128)(2,1)}, bf16[288,576]{1,0:T(8,128)(2,1)S(1)}, u32[]{:S(2)}) copy-start(bf16[288,576]{1,0:T(8,128)(2,1)S(1)} %collective-permute-done.3) | copy-start | bytes 995332
  82.3 15.8 %collective-permute-start.4 = (bf16[288,576]{1,0:T(8,128)(2,1)S(1)}, bf16[288,576]{1,0:T(8,128)(2,1)S(1)}, u32[]{:S(2)}, u32[]{:S(2)}) collective-permute-start(bf16[288,576]{1,0:T(8,128)(2,1)S(1)} %collective-permute-done.3), channel_id=1, source_target_pairs={{0,1},{1,2},{2,3},{3,4},{4,5},{5,6},{6,7},{7,0},{8,9},{9,10},{10,1... | collective-permute-start | bytes 995336 | tf_op jit(solution)/shard_map/ppermute | solution.py:97
  90.2 24.1 %copy-start.30 = (bf16[288,576]{1,0:T(8,128)(2,1)}, bf16[288,576]{1,0:T(8,128)(2,1)S(1)}, u32[]{:S(2)}) copy-start(bf16[288,576]{1,0:T(8,128)(2,1)S(1)} %collective-permute-done.11) | copy-start | bytes 995332
  90.2 15.8 %collective-permute-start.12 = (bf16[288,576]{1,0:T(8,128)(2,1)S(1)}, bf16[288,576]{1,0:T(8,128)(2,1)S(1)}, u32[]{:S(2)}, u32[]{:S(2)}) collective-permute-start(bf16[288,576]{1,0:T(8,128)(2,1)S(1)} %collective-permute-done.11), channel_id=1, source_target_pairs={{0,1},{1,2},{2,3},{3,4},{4,5},{5,6},{6,7},{7,0},{8,9},{9,10},{10,1... | collective-permute-start | bytes 995336 | tf_op jit(solution)/shard_map/ppermute | solution.py:97
  98.1 17.1 %copy-start.29 = (bf16[288,576]{1,0:T(8,128)(2,1)}, bf16[288,576]{1,0:T(8,128)(2,1)S(1)}, u32[]{:S(2)}) copy-start(bf16[288,576]{1,0:T(8,128)(2,1)S(1)} %collective-permute-done.4) | copy-start | bytes 995332
  98.1 15.9 %collective-permute-start.5 = (bf16[288,576]{1,0:T(8,128)(2,1)S(1)}, bf16[288,576]{1,0:T(8,128)(2,1)}, u32[]{:S(2)}, u32[]{:S(2)}) collective-permute-start(bf16[288,576]{1,0:T(8,128)(2,1)S(1)} %collective-permute-done.4), channel_id=1, source_target_pairs={{0,1},{1,2},{2,3},{3,4},{4,5},{5,6},{6,7},{7,0},{8,9},{9,10},{10,1... | collective-permute-start | bytes 995336 | tf_op jit(solution)/shard_map/ppermute | solution.py:97
  106.0 9.2 %copy-start.31 = (bf16[288,576]{1,0:T(8,128)(2,1)}, bf16[288,576]{1,0:T(8,128)(2,1)S(1)}, u32[]{:S(2)}) copy-start(bf16[288,576]{1,0:T(8,128)(2,1)S(1)} %collective-permute-done.12) | copy-start | bytes 995332
  106.0 15.9 %collective-permute-start.13 = (bf16[288,576]{1,0:T(8,128)(2,1)S(1)}, bf16[288,576]{1,0:T(8,128)(2,1)}, u32[]{:S(2)}, u32[]{:S(2)}) collective-permute-start(bf16[288,576]{1,0:T(8,128)(2,1)S(1)} %collective-permute-done.12), channel_id=1, source_target_pairs={{0,1},{1,2},{2,3},{3,4},{4,5},{5,6},{6,7},{7,0},{8,9},{9,10},{10,1... | collective-permute-start | bytes 995336 | tf_op jit(solution)/shard_map/ppermute | solution.py:97
  114.0 15.5 %collective-permute-start.6 = (bf16[288,576]{1,0:T(8,128)(2,1)}, bf16[288,576]{1,0:T(8,128)(2,1)}, u32[]{:S(2)}, u32[]{:S(2)}) collective-permute-start(bf16[288,576]{1,0:T(8,128)(2,1)} %collective-permute-done.5), channel_id=1, source_target_pairs={{0,1},{1,2},{2,3},{3,4},{4,5},{5,6},{6,7},{7,0},{8,9},{9,10},{10,1... | collective-permute-start | bytes 995336 | tf_op jit(solution)/shard_map/ppermute | solution.py:97
  115.2 64.4 %copy-start.12 = (f32[96,64]{1,0:T(8,128)}, f32[96,64]{1,0:T(8,128)S(1)}, u32[]{:S(2)}) copy-start(f32[96,64]{1,0:T(8,128)S(1)} %get-tuple-element.51) | copy-start | bytes 73732
  115.2 14.3 %copy-start.5 = (bf16[288,576]{1,0:T(8,128)(2,1)S(1)}, bf16[288,576]{1,0:T(8,128)(2,1)}, u32[]{:S(2)}) copy-start(bf16[288,576]{1,0:T(8,128)(2,1)} %param.18) | copy-start | bytes 995332
  129.5 11.7 %copy-start.47 = (f32[4608]{0:T(1024)S(1)}, f32[4608]{0:T(1024)}, u32[]{:S(2)}) copy-start(f32[4608]{0:T(1024)} %param.22) | copy-start | bytes 55300
  164.3 18.9 %copy-start.17 = (bf16[3,96,2,128]{3,2,1,0:T(2,128)(2,1)}, bf16[3,96,2,128]{3,2,1,0:T(2,128)(2,1)S(1)}, u32[]{:S(2)}) copy-start(bf16[3,96,2,128]{3,2,1,0:T(2,128)(2,1)S(1)} %convert_element_type.140) | copy-start | bytes 442372
  195.8 160.5 %reduce-scatter.12.cloned.1.call-start = ((), (), s32[]{:S(2)}) async-start(), calls=%async_computation.11 | async-start | bytes 3981312
  216.1 163.4 %copy-start.4 = (bf16[288,576]{1,0:T(8,128)(2,1)S(1)}, bf16[288,576]{1,0:T(8,128)(2,1)}, u32[]{:S(2)}) copy-start(bf16[288,576]{1,0:T(8,128)(2,1)} %param.19) | copy-start | bytes 995332
  216.1 166.1 %copy-start.52 = (s32[3]{0:T(128)S(1)}, s32[3]{0:T(128)}, u32[]{:S(2)}) copy-start(s32[3]{0:T(128)} %param.20) | copy-start | bytes 40
  216.1 282.2 %all-gather.15.cloned.1.call-start = ((), (), s32[]{:S(2)}) async-start(), calls=%async_computation.9 | async-start | bytes 3317760 | tf_op jit(solution)/shard_map/all_gather | solution.py:260
  442.9 109.1 %reduce-scatter.8.cloned.1.call-start = ((), (), s32[]{:S(2)}) async-start(), calls=%async_computation.7 | async-start | bytes 1474560 | tf_op jit(solution)/shard_map/reduce_scatter | solution.py:322
  527.5 59.0 %all-reduce.5.cloned.1.call-start = ((), (), s32[]{:S(2)}) async-start(), calls=%async_computation.8 | async-start | bytes 131072 | tf_op jit(solution)/shard_map/psum | solution.py:297
  531.4 182.5 %all-reduce.7.cloned.1.call-start = ((), (), s32[]{:S(2)}) async-start(), calls=%async_computation.12 | async-start | bytes 5898240 | tf_op jit(solution)/shard_map/psum | solution.py:339
  542.0 171.9 %copy-start.6 = (bf16[288,576]{1,0:T(8,128)(2,1)S(1)}, bf16[288,576]{1,0:T(8,128)(2,1)}, u32[]{:S(2)}) copy-start(bf16[288,576]{1,0:T(8,128)(2,1)} %param.18) | copy-start | bytes 995332
  542.0 194.5 %copy-start.49 = (f32[288]{0:T(512)S(1)}, f32[288]{0:T(512)}, u32[]{:S(2)}) copy-start(f32[288]{0:T(512)} %copy-done.48) | copy-start | bytes 3460
  542.0 194.5 %copy-start.50 = (f32[288]{0:T(512)S(1)}, f32[288]{0:T(512)}, u32[]{:S(2)}) copy-start(f32[288]{0:T(512)} %get-tuple-element.45) | copy-start | bytes 3460
  (31 other events, 99.1 us)
Sparse Core Ops, SparseCore 0:
  9.6 26.7 all-gather.8
  37.9 27.1 all-gather.6
  66.7 37.4 all-gather.10
  105.6 37.4 all-gather.12
  195.9 77.8 reduce-scatter.9
  277.2 79.0 reduce-scatter.11
  443.0 55.2 all-gather.14
  527.6 24.3 reduce-scatter.7
  554.8 31.5 all-reduce.4
  589.9 123.9 all-reduce.6
